TPU v7x, 32 devices: a whole 2x2x4 slice. The times are simulated.
32 devices in a mesh: seq: 4 (over y, x), exp: 8 (over z, core).
Axes of the slice: x: 2, y: 2, z: 4, core: 2. Of those that a mesh axis runs over, the one named last changes fastest.
Arguments:
- tokens: bfloat16 [2, 24576, 1024], P(None, ('seq', 'exp')), may hold values from -60 to 60
- router: bfloat16 [1024, 64], replicated, may hold values from -0.25 to 0.25
- w_in: bfloat16 [16, 1024, 4096], P('exp', None, 'seq'), may hold values from -0.1875 to 0.1875
- w_out: bfloat16 [16, 4096, 1024], P('exp', 'seq'), may hold values from -0.09375 to 0.09375
- grad_out: bfloat16 [2, 24576, 1024], P(None, ('seq', 'exp')), may hold values from -6 to 6
Outputs:
- mixed: bfloat16 [2, 24576, 1024], P(None, ('seq', 'exp'))
- grad_tokens: bfloat16 [2, 24576, 1024], P(None, ('seq', 'exp'))
- grad_router: float32 [1024, 64], P(('seq', 'exp'))
- grad_w_in: bfloat16 [16, 1024, 4096], P('exp', None, 'seq')
- grad_w_out: bfloat16 [16, 4096, 1024], P('exp', 'seq')
All inputs are finite; a program needn't handle non-finite values.
Results may differ from a plain program's by a relative error of at most 0.018.
Values may be sent and summed in bfloat16 or wider, within the bound.
A program may use at most 128 MiB of HBM per device.

v0:
```python
import jax
import jax.numpy as jnp
from jax import lax
from jax.sharding import PartitionSpec as P


def on_device(tokens, router, w_in, w_out, grad_out):
    clips, tok_rows, width = tokens.shape
    slot_total = router.shape[1]
    owned = slot_total // lax.axis_size("exp")
    experts_here = w_in.shape[0]
    per_expert = owned // experts_here
    logits = jnp.dot(
        tokens.reshape(clips * tok_rows, width), router, preferred_element_type=jnp.float32
    ).reshape(clips, tok_rows, slot_total)
    slot_peak = lax.pmax(jnp.max(logits, axis=1), ("seq", "exp"))
    exp_terms = jnp.exp(logits - slot_peak[:, None, :])
    slot_mass = lax.psum(jnp.sum(exp_terms, axis=1), ("seq", "exp"))
    dispatch = exp_terms / slot_mass[:, None, :]
    dispatch_b = dispatch.astype(jnp.bfloat16)
    mixing = jax.nn.softmax(logits, axis=2)
    mixing_b = mixing.astype(jnp.bfloat16)
    inputs = jnp.einsum("cts,ctd->scd", dispatch_b, tokens, preferred_element_type=jnp.float32)
    grads = jnp.einsum("cts,ctd->scd", mixing_b, grad_out, preferred_element_type=jnp.float32)
    summed = lax.psum(jnp.concatenate([inputs, grads], axis=1), ("seq", "exp"))
    owner_sums = lax.dynamic_slice_in_dim(summed, lax.axis_index("exp") * owned, owned, 0)
    expert_rows = (
        owner_sums[:, :clips].astype(jnp.bfloat16).reshape(experts_here, per_expert * clips, width)
    )
    grad_rows = (
        owner_sums[:, clips:].astype(jnp.bfloat16).reshape(experts_here, per_expert * clips, width)
    )
    pre = jnp.einsum("erd,edh->erh", expert_rows, w_in, preferred_element_type=jnp.float32)
    hidden = jax.nn.gelu(pre).astype(jnp.bfloat16)
    expert_part = jnp.einsum("erh,ehd->erd", hidden, w_out, preferred_element_type=jnp.float32)
    hidden_grad = jnp.einsum("erd,ehd->erh", grad_rows, w_out, preferred_element_type=jnp.float32)
    pre_grad = jax.vjp(jax.nn.gelu, pre)[1](hidden_grad)[0].astype(jnp.bfloat16)
    grad_w_out = jnp.einsum(
        "erh,erd->ehd", hidden, grad_rows, preferred_element_type=jnp.float32
    ).astype(jnp.bfloat16)
    grad_w_in = jnp.einsum(
        "erd,erh->edh", expert_rows, pre_grad, preferred_element_type=jnp.float32
    ).astype(jnp.bfloat16)
    input_part = jnp.einsum("erh,edh->erd", pre_grad, w_in, preferred_element_type=jnp.float32)
    out_sums, in_sums = (
        lax.psum(expert_part.astype(jnp.bfloat16), "seq").astype(jnp.float32),
        lax.psum(input_part.astype(jnp.bfloat16), "seq").astype(jnp.float32),
    )
    slot_outputs = out_sums.astype(jnp.bfloat16).reshape(owned, clips, width)
    slot_in_grads = in_sums.astype(jnp.bfloat16).reshape(owned, clips, width)
    shard_rows = lax.all_gather(slot_outputs, "exp", axis=0, tiled=True)
    weights = mixing_b
    outputs = jnp.einsum("cts,scd->ctd", weights, shard_rows, preferred_element_type=jnp.float32)
    block = jnp.einsum("ctd,scd->cts", grad_out, shard_rows, preferred_element_type=jnp.float32)
    mixed = outputs
    mixing_grad = block
    shard_rows = lax.all_gather(slot_in_grads, "exp", axis=0, tiled=True)
    weights = dispatch_b
    outputs = jnp.einsum("cts,scd->ctd", weights, shard_rows, preferred_element_type=jnp.float32)
    block = jnp.einsum("ctd,scd->cts", tokens, shard_rows, preferred_element_type=jnp.float32)
    inner = lax.psum(jnp.sum(dispatch * block, axis=1), ("seq", "exp"))
    logit_grad = dispatch * (block - inner[:, None, :]) + mixing * (
        mixing_grad - jnp.sum(mixing * mixing_grad, axis=2, keepdims=True)
    )
    logit_b = logit_grad.astype(jnp.bfloat16)
    router_part = jnp.dot(
        logit_b.reshape(clips * tok_rows, slot_total), router.T, preferred_element_type=jnp.float32
    ).reshape(clips, tok_rows, width)
    grad_tokens = (outputs + router_part).astype(jnp.bfloat16)
    grad_router = lax.psum_scatter(
        jnp.einsum("ctd,cts->ds", tokens, logit_b, preferred_element_type=jnp.float32),
        ("seq", "exp"),
        scatter_dimension=0,
        tiled=True,
    )
    return (mixed.astype(jnp.bfloat16), grad_tokens, grad_router, grad_w_in, grad_w_out)


def solution(mesh):
    return jax.shard_map(
        on_device,
        mesh=mesh,
        in_specs=(
            P(None, ("seq", "exp"), None),
            P(),
            P("exp", None, "seq"),
            P("exp", "seq", None),
            P(None, ("seq", "exp"), None),
        ),
        out_specs=(
            P(None, ("seq", "exp"), None),
            P(None, ("seq", "exp"), None),
            P(("seq", "exp"), None),
            P("exp", None, "seq"),
            P("exp", "seq", None),
        ),
        check_vma=False,
    )
```

profile of v0, /device:TPU:0, one launch (start us, length us, event | category | flops | bytes accessed | tf_op | source)
XLA Modules:
  0.0 442.6 jit_solution(9276342582157628203)
XLA Ops:
  7.2 1.8 copy-done
  9.1 2.1 fusion.37
  12.0 41.9 %pmax.7 = f32[2,64]{1,0:T(2,128)S(1)} all-reduce(f32[2,64]{1,0:T(2,128)S(1)} %get-tuple-element.26), channel_id=1, replica_groups=mesh['seq'=4,'exp'=8] {'seq','exp'}, use_global_device_ids=true, to_apply=%region_3.0 | all-reduce | flops 128 | bytes 1024 | tf_op jit(solution)/shard_map/pmax | solution.py:16
  54.7 40.3 %psum.35 = f32[2,64]{1,0:T(2,128)S(1)} all-reduce(f32[2,64]{1,0:T(2,128)} %fusion.13), channel_id=1, replica_groups=mesh['seq'=4,'exp'=8] {'seq','exp'}, use_global_device_ids=true, to_apply=%region_5.0 | all-reduce | flops 128 | bytes 1024 | tf_op jit(solution)/shard_map/psum | solution.py:18
  96.5 3.4 convolution_bitcast_fusion
  99.9 2.4 pad_maximum_fusion
  102.3 49.9 %all-reduce.5 = bf16[64,4,1024]{2,0,1:T(8,128)(2,1)} all-reduce(f32[64,4,1024]{2,0,1:T(8,128)} %pad_maximum_fusion), channel_id=1, replica_groups=mesh['seq'=4,'exp'=8] {'seq','exp'}, use_global_device_ids=true, to_apply=%region_6.0 | all-reduce | flops 262144 | bytes 1572864 | tf_op jit(solution)/shard_map/psum | solution.py:25
  158.4 3.5 fusion.38
  162.0 3.5 fusion.28
  170.1 4.0 convolution_convert_fusion.3
  177.0 4.2 convolution_convert_fusion
  181.2 3.3 convolution_convert_fusion.1
  184.5 33.1 %all-reduce.4.cloned.1.call-done = (bf16[8,2,1024]{2,0,1:T(8,128)(2,1)}, bf16[8,2,1024]{2,0,1:T(8,128)(2,1)}) async-done(((bf16[8,2,1024]{2,0,1:T(8,128)(2,1)}, bf16[8,2,1024]{2,0,1:T(8,128)(2,1)}), (bf16[8,2,1024]{2,0,1:T(8,128)(2,1)}, bf16[8,2,1024]{2,0,1:T(8,128)(2,1)})) %all-reduce.4.cloned.1.call-update) | async-done | bytes 65552 | tf_op jit(solution)/shard_map/psum | solution.py:46
  217.6 14.6 %all_gather.7 = bf16[64,2,1024]{2,0,1:T(8,128)(2,1)S(1)} all-gather(bf16[8,2,1024]{2,0,1:T(8,128)(2,1)} %get-tuple-element.21), channel_id=1, replica_groups=mesh['seq'=4,'exp'=8] {'exp'}, dimensions={0}, use_global_device_ids=true | all-gather | bytes 294912 | tf_op jit(solution)/shard_map/all_gather | solution.py:57
  232.2 3.8 fusion.17
  236.0 2.4 multiply_reduce_fusion.1
  238.4 14.2 %all_gather.6 = bf16[64,2,1024]{2,0,1:T(8,128)(2,1)S(1)} all-gather(bf16[8,2,1024]{2,0,1:T(8,128)(2,1)S(1)} %copy-done.8), channel_id=1, replica_groups=mesh['seq'=4,'exp'=8] {'exp'}, dimensions={0}, use_global_device_ids=true | all-gather | bytes 294912 | tf_op jit(solution)/shard_map/all_gather | solution.py:51
  252.6 1.8 convolution_bitcast_fusion.2
  254.4 39.4 %psum.39 = f32[2,64]{1,0:T(2,128)} all-reduce(f32[2,64]{1,0:T(2,128)} %get-tuple-element.30), channel_id=1, replica_groups=mesh['seq'=4,'exp'=8] {'seq','exp'}, use_global_device_ids=true, to_apply=%region_10.0 | all-reduce | flops 128 | bytes 1024 | tf_op jit(solution)/shard_map/psum | solution.py:61
  293.8 3.0 convolution_bitcast_fusion.4
  296.8 2.0 copy.23
  298.8 3.7 convolution_convert_fusion.2
  302.5 6.2 %add_convert_fusion = bf16[2,768,1024]{2,1,0:T(8,128)(2,1)} fusion(f32[2,768,1024]{2,1,0:T(8,128)} %fusion.17, f32[2,768,64]{1,2,0:T(8,128)} %convolution_bitcast_fusion.2, f32[2,768,64]{1,2,0:T(8,128)} %get-tuple-element.31, f32[2,64]{1,0:T(2,128)} %psum.39, bf16[1024,64]{0,1:T(8,128)(2,1)} %param.6, f32[2,768,64]{1,2,0:T(8,128)} %get-tuple-element.25, ...), kind=kOutput, calls=%fused_computation.2 | convolution fusion | flops 205555264 | bytes 11148800 | tf_op jit(solution)/shard_map/dot_general | solution.py:66
  308.7 127.1 %reduce-scatter.4.cloned.1.call-done = f32[32,64]{1,0:T(8,128)} async-done(((f32[1024,64]{1,0:T(8,128)}), f32[32,64]{1,0:T(8,128)}) %reduce-scatter.4.cloned.1.call-update) | async-done | bytes 8208
  (35 shorter events, 16.9 us)
Async XLA Ops:
  7.2 1.9 copy-start
  7.2 210.4 %all-reduce.4.cloned.1.call-start = ((), (), s32[]{:S(2)}) async-start(), calls=%async_computation.2 | async-start | bytes 131072 | tf_op jit(solution)/shard_map/psum | solution.py:46
  158.4 3.5 copy-start.6
  158.4 7.7 %copy-start.1 = (bf16[2,1024,1024]{2,1,0:T(8,128)(2,1)S(1)}, bf16[2,1024,1024]{2,1,0:T(8,128)(2,1)}, u32[]{:S(2)}) copy-start(bf16[2,1024,1024]{2,1,0:T(8,128)(2,1)} %param.8) | copy-start | bytes 12582916
  165.5 0.6 copy-start.4
  176.9 258.9 %reduce-scatter.4.cloned.1.call-start = ((), (), s32[]{:S(2)}) async-start(), calls=%async_computation.1 | async-start | bytes 540672
  177.0 4.2 copy-start.5
  177.0 4.2 copy-start.7
  232.2 6.2 %copy-start.8 = (bf16[8,2,1024]{2,0,1:T(8,128)(2,1)S(1)}, bf16[8,2,1024]{2,0,1:T(8,128)(2,1)}, u32[]{:S(2)}) copy-start(bf16[8,2,1024]{2,0,1:T(8,128)(2,1)} %get-tuple-element.20) | copy-start | bytes 98308
  232.2 20.4 %copy-start.2 = (bf16[2,768,1024]{2,1,0:T(8,128)(2,1)S(1)}, bf16[2,768,1024]{2,1,0:T(8,128)(2,1)}, u32[]{:S(2)}) copy-start(bf16[2,768,1024]{2,1,0:T(8,128)(2,1)} %param.9) | copy-start | bytes 9437188
  252.6 1.8 copy-start.3
Sparse Core Ops, SparseCore 0:
  177.0 40.5 all-reduce.3
  298.9 136.8 reduce-scatter.3
where the time goes:
time: 444 us; the launch traced here: 443 us
  blocking collectives  200 us (45%)
  waiting for transfers between devices  160 us (36%)
  matrix products  47.6 us (11%)
  local copies, waits for them, and re-layouts  16.2 us (4%)
  between operations  14.1 us (3%)
    unnamed x3, waiting for transfers between devices  127 us
    psum x1, blocking collectives, on_device(): summed = lax.psum(jnp.concatenate([inputs, grads], axis=1), ('seq', 'exp'))  49.9 us
    pmax x1, blocking collectives, on_device(): slot_peak = lax.pmax(jnp.max(logits, axis=1), ('seq', 'exp'))  41.9 us
    psum x1, blocking collectives, on_device(): slot_mass = lax.psum(jnp.sum(exp_terms, axis=1), ('seq', 'exp'))  40.3 us
    psum x1, blocking collectives, on_device(): inner = lax.psum(jnp.sum(dispatch * block, axis=1), ('seq', 'exp'))  39.4 us
    psum x1, waiting for transfers between devices, on_device(): lax.psum(expert_part.astype(jnp.bfloat16), 'seq').astype(jnp.float32)  33.1 us
    all_gather x1, blocking collectives, on_device(): shard_rows = lax.all_gather(slot_in_grads, 'exp', axis=0, tiled=True)  14.6 us
    all_gather x1, blocking collectives, on_device(): shard_rows = lax.all_gather(slot_outputs, 'exp', axis=0, tiled=True)  14.2 us
  transfers between devices with their start and end apart: 2, of which 2 were waited for; matrix products, arithmetic and copies ran while one was open for 4% of the time, Pallas kernels for 0%

commit v1 on v0

--- a/solution.py
+++ b/solution.py
@@ -58,7 +58,7 @@
     weights = dispatch_b
     outputs = jnp.einsum("cts,scd->ctd", weights, shard_rows, preferred_element_type=jnp.float32)
     block = jnp.einsum("ctd,scd->cts", tokens, shard_rows, preferred_element_type=jnp.float32)
-    inner = lax.psum(jnp.sum(dispatch * block, axis=1), ("seq", "exp"))
+    inner = lax.psum(lax.psum(jnp.sum(dispatch * block, axis=1), "exp"), "seq")
     logit_grad = dispatch * (block - inner[:, None, :]) + mixing * (
         mixing_grad - jnp.sum(mixing * mixing_grad, axis=2, keepdims=True)
     )

time: 444 us -> 428 us (0.964)
  blocking collectives: 200 us -> 188 us
    psum x1 -> x2, blocking collectives: 39.4 us -> 27.1 us  [on_device(): inner = lax.psum(lax.psum(jnp.sum(dispatch * block, axis=1), 'exp'), 'seq')]
where the time goes in v1:
time: 428 us; the launch traced here: 426 us
  blocking collectives  188 us (44%)
  waiting for transfers between devices  156 us (36%)
  matrix products  47.6 us (11%)
  local copies, waits for them, and re-layouts  16.2 us (4%)
  between operations  14.1 us (3%)
    unnamed x3, waiting for transfers between devices  123 us
    psum x1, blocking collectives, on_device(): summed = lax.psum(jnp.concatenate([inputs, grads], axis=1), ('seq', 'exp'))  49.9 us
    pmax x1, blocking collectives, on_device(): slot_peak = lax.pmax(jnp.max(logits, axis=1), ('seq', 'exp'))  41.9 us
    psum x1, blocking collectives, on_device(): slot_mass = lax.psum(jnp.sum(exp_terms, axis=1), ('seq', 'exp'))  40.3 us
    psum x1, waiting for transfers between devices, on_device(): lax.psum(expert_part.astype(jnp.bfloat16), 'seq').astype(jnp.float32)  33.1 us
    psum x2, blocking collectives, on_device(): inner = lax.psum(lax.psum(jnp.sum(dispatch * block, axis=1), 'exp'), 'seq')  27.1 us
    all_gather x1, blocking collectives, on_device(): shard_rows = lax.all_gather(slot_in_grads, 'exp', axis=0, tiled=True)  14.6 us
    all_gather x1, blocking collectives, on_device(): shard_rows = lax.all_gather(slot_outputs, 'exp', axis=0, tiled=True)  14.2 us
  transfers between devices with their start and end apart: 2, of which 2 were waited for; matrix products, arithmetic and copies ran while one was open for 4% of the time, Pallas kernels for 0%

profile of v1, /device:TPU:0, one launch (start us, length us, event | category | flops | bytes accessed | tf_op | source)
XLA Modules:
  0.0 426.5 jit_solution(11053511454242505366)
XLA Ops:
  7.2 1.8 copy-done
  9.1 2.1 fusion.37
  12.0 41.9 %pmax.7 = f32[2,64]{1,0:T(2,128)S(1)} all-reduce(f32[2,64]{1,0:T(2,128)S(1)} %get-tuple-element.26), channel_id=1, replica_groups=mesh['seq'=4,'exp'=8] {'seq','exp'}, use_global_device_ids=true, to_apply=%region_3.0 | all-reduce | flops 128 | bytes 1024 | tf_op jit(solution)/shard_map/pmax | solution.py:16
  54.7 40.3 %psum.42 = f32[2,64]{1,0:T(2,128)S(1)} all-reduce(f32[2,64]{1,0:T(2,128)} %fusion.13), channel_id=1, replica_groups=mesh['seq'=4,'exp'=8] {'seq','exp'}, use_global_device_ids=true, to_apply=%region_5.0 | all-reduce | flops 128 | bytes 1024 | tf_op jit(solution)/shard_map/psum | solution.py:18
  96.5 3.4 convolution_bitcast_fusion
  99.9 2.4 pad_maximum_fusion
  102.3 49.9 %all-reduce.5 = bf16[64,4,1024]{2,0,1:T(8,128)(2,1)} all-reduce(f32[64,4,1024]{2,0,1:T(8,128)} %pad_maximum_fusion), channel_id=1, replica_groups=mesh['seq'=4,'exp'=8] {'seq','exp'}, use_global_device_ids=true, to_apply=%region_6.0 | all-reduce | flops 262144 | bytes 1572864 | tf_op jit(solution)/shard_map/psum | solution.py:25
  158.4 3.5 fusion.38
  162.0 3.5 fusion.28
  170.1 4.0 convolution_convert_fusion.3
  177.0 4.2 convolution_convert_fusion
  181.2 3.3 convolution_convert_fusion.1
  184.5 33.1 %all-reduce.4.cloned.1.call-done = (bf16[8,2,1024]{2,0,1:T(8,128)(2,1)}, bf16[8,2,1024]{2,0,1:T(8,128)(2,1)}) async-done(((bf16[8,2,1024]{2,0,1:T(8,128)(2,1)}, bf16[8,2,1024]{2,0,1:T(8,128)(2,1)}), (bf16[8,2,1024]{2,0,1:T(8,128)(2,1)}, bf16[8,2,1024]{2,0,1:T(8,128)(2,1)})) %all-reduce.4.cloned.1.call-update) | async-done | bytes 65552 | tf_op jit(solution)/shard_map/psum | solution.py:46
  217.6 14.6 %all_gather.7 = bf16[64,2,1024]{2,0,1:T(8,128)(2,1)S(1)} all-gather(bf16[8,2,1024]{2,0,1:T(8,128)(2,1)} %get-tuple-element.21), channel_id=1, replica_groups=mesh['seq'=4,'exp'=8] {'exp'}, dimensions={0}, use_global_device_ids=true | all-gather | bytes 294912 | tf_op jit(solution)/shard_map/all_gather | solution.py:57
  232.2 3.8 fusion.17
  236.0 2.4 multiply_reduce_fusion.1
  238.4 14.2 %all_gather.6 = bf16[64,2,1024]{2,0,1:T(8,128)(2,1)S(1)} all-gather(bf16[8,2,1024]{2,0,1:T(8,128)(2,1)S(1)} %copy-done.8), channel_id=1, replica_groups=mesh['seq'=4,'exp'=8] {'exp'}, dimensions={0}, use_global_device_ids=true | all-gather | bytes 294912 | tf_op jit(solution)/shard_map/all_gather | solution.py:51
  254.4 17.5 %psum.46 = f32[2,64]{1,0:T(2,128)} all-reduce(f32[2,64]{1,0:T(2,128)} %get-tuple-element.30), channel_id=1, replica_groups=mesh['seq'=4,'exp'=8] {'exp'}, use_global_device_ids=true, to_apply=%region_10.0 | all-reduce | flops 128 | bytes 1024 | tf_op jit(solution)/shard_map/psum | solution.py:61
  271.9 9.6 %psum.47 = f32[2,64]{1,0:T(2,128)} all-reduce(f32[2,64]{1,0:T(2,128)} %psum.46), channel_id=1, replica_groups=mesh['seq'=4,'exp'=8] {'seq'}, use_global_device_ids=true, to_apply=%region_11.0 | all-reduce | flops 128 | bytes 1024 | tf_op jit(solution)/shard_map/psum | solution.py:61
  281.5 3.0 convolution_bitcast_fusion.4
  284.6 2.0 copy.23
  286.6 3.7 convolution_convert_fusion.2
  290.2 6.2 %add_convert_fusion = bf16[2,768,1024]{2,1,0:T(8,128)(2,1)} fusion(f32[2,768,1024]{2,1,0:T(8,128)} %fusion.17, f32[2,768,64]{1,2,0:T(8,128)} %convolution_bitcast_fusion.2, f32[2,768,64]{1,2,0:T(8,128)} %get-tuple-element.31, f32[2,64]{1,0:T(2,128)} %psum.47, bf16[1024,64]{0,1:T(8,128)(2,1)} %param.6, f32[2,768,64]{1,2,0:T(8,128)} %get-tuple-element.25, ...), kind=kOutput, calls=%fused_computation.2 | convolution fusion | flops 205555264 | bytes 11148800 | tf_op jit(solution)/shard_map/dot_general | solution.py:66
  296.5 123.2 %reduce-scatter.4.cloned.1.call-done = f32[32,64]{1,0:T(8,128)} async-done(((f32[1024,64]{1,0:T(8,128)}), f32[32,64]{1,0:T(8,128)}) %reduce-scatter.4.cloned.1.call-update) | async-done | bytes 8208
  (36 shorter events, 18.8 us)
Async XLA Ops:
  7.2 1.9 copy-start
  7.2 210.4 %all-reduce.4.cloned.1.call-start = ((), (), s32[]{:S(2)}) async-start(), calls=%async_computation.2 | async-start | bytes 131072 | tf_op jit(solution)/shard_map/psum | solution.py:46
  158.4 3.5 copy-start.6
  158.4 7.7 %copy-start.1 = (bf16[2,1024,1024]{2,1,0:T(8,128)(2,1)S(1)}, bf16[2,1024,1024]{2,1,0:T(8,128)(2,1)}, u32[]{:S(2)}) copy-start(bf16[2,1024,1024]{2,1,0:T(8,128)(2,1)} %param.8) | copy-start | bytes 12582916
  165.5 0.6 copy-start.4
  176.9 242.7 %reduce-scatter.4.cloned.1.call-start = ((), (), s32[]{:S(2)}) async-start(), calls=%async_computation.1 | async-start | bytes 540672
  177.0 4.2 copy-start.5
  177.0 4.2 copy-start.7
  232.2 6.2 %copy-start.8 = (bf16[8,2,1024]{2,0,1:T(8,128)(2,1)S(1)}, bf16[8,2,1024]{2,0,1:T(8,128)(2,1)}, u32[]{:S(2)}) copy-start(bf16[8,2,1024]{2,0,1:T(8,128)(2,1)} %get-tuple-element.20) | copy-start | bytes 98308
  232.2 20.4 %copy-start.2 = (bf16[2,768,1024]{2,1,0:T(8,128)(2,1)S(1)}, bf16[2,768,1024]{2,1,0:T(8,128)(2,1)}, u32[]{:S(2)}) copy-start(bf16[2,768,1024]{2,1,0:T(8,128)(2,1)} %param.9) | copy-start | bytes 9437188
  252.6 1.8 copy-start.3
Sparse Core Ops, SparseCore 0:
  177.0 40.5 all-reduce.3
  286.7 132.8 reduce-scatter.3

commit v2 on v0

--- a/solution.py
+++ b/solution.py
@@ -58,7 +58,7 @@
     weights = dispatch_b
     outputs = jnp.einsum("cts,scd->ctd", weights, shard_rows, preferred_element_type=jnp.float32)
     block = jnp.einsum("ctd,scd->cts", tokens, shard_rows, preferred_element_type=jnp.float32)
-    inner = lax.psum(jnp.sum(dispatch * block, axis=1), ("seq", "exp"))
+    inner = jnp.sum(lax.all_gather(jnp.sum(dispatch * block, axis=1), ("seq", "exp")), axis=0)
     logit_grad = dispatch * (block - inner[:, None, :]) + mixing * (
         mixing_grad - jnp.sum(mixing * mixing_grad, axis=2, keepdims=True)
     )

time: 444 us -> 445 us (level)
    all_gather x0 -> x1, blocking collectives: none -> 43.1 us  [on_device(): lax.all_gather(jnp.sum(dispatch * block, axis=1), ('seq', 'exp'))]
    psum x1 -> x0, blocking collectives: 39.4 us -> none  [on_device(): inner = lax.psum(jnp.sum(dispatch * block, axis=1), ('seq', 'exp'))]
where the time goes in v2:
time: 445 us; the launch traced here: 443 us
  blocking collectives  204 us (46%)
  waiting for transfers between devices  156 us (35%)
  matrix products  47.1 us (11%)
  local copies, waits for them, and re-layouts  16.2 us (4%)
  between operations  14.1 us (3%)
  other arithmetic  5.42 us (1%)
    unnamed x3, waiting for transfers between devices  123 us
    psum x1, blocking collectives, on_device(): summed = lax.psum(jnp.concatenate([inputs, grads], axis=1), ('seq', 'exp'))  49.9 us
    all_gather x1, blocking collectives, on_device(): lax.all_gather(jnp.sum(dispatch * block, axis=1), ('seq', 'exp'))  43.1 us
    pmax x1, blocking collectives, on_device(): slot_peak = lax.pmax(jnp.max(logits, axis=1), ('seq', 'exp'))  41.9 us
    psum x1, blocking collectives, on_device(): slot_mass = lax.psum(jnp.sum(exp_terms, axis=1), ('seq', 'exp'))  40.3 us
    psum x1, waiting for transfers between devices, on_device(): lax.psum(expert_part.astype(jnp.bfloat16), 'seq').astype(jnp.float32)  33.1 us
    all_gather x1, blocking collectives, on_device(): shard_rows = lax.all_gather(slot_in_grads, 'exp', axis=0, tiled=True)  14.6 us
    all_gather x1, blocking collectives, on_device(): shard_rows = lax.all_gather(slot_outputs, 'exp', axis=0, tiled=True)  14.2 us
  transfers between devices with their start and end apart: 2, of which 2 were waited for; matrix products, arithmetic and copies ran while one was open for 4% of the time, Pallas kernels for 0%

profile of v2, /device:TPU:0, one launch (start us, length us, event | category | flops | bytes accessed | tf_op | source)
XLA Modules:
  0.0 443.2 jit_solution(3502107462263146335)
XLA Ops:
  7.2 1.8 copy-done
  9.1 2.1 fusion.37
  12.0 41.9 %pmax.7 = f32[2,64]{1,0:T(2,128)S(1)} all-reduce(f32[2,64]{1,0:T(2,128)S(1)} %get-tuple-element.26), channel_id=1, replica_groups=mesh['seq'=4,'exp'=8] {'seq','exp'}, use_global_device_ids=true, to_apply=%region_3.0 | all-reduce | flops 128 | bytes 1024 | tf_op jit(solution)/shard_map/pmax | solution.py:16
  54.7 40.3 %psum.28 = f32[2,64]{1,0:T(2,128)S(1)} all-reduce(f32[2,64]{1,0:T(2,128)} %fusion.13), channel_id=1, replica_groups=mesh['seq'=4,'exp'=8] {'seq','exp'}, use_global_device_ids=true, to_apply=%region_5.0 | all-reduce | flops 128 | bytes 1024 | tf_op jit(solution)/shard_map/psum | solution.py:18
  96.5 3.4 convolution_bitcast_fusion
  99.9 2.4 pad_maximum_fusion
  102.3 49.9 %all-reduce.5 = bf16[64,4,1024]{2,0,1:T(8,128)(2,1)} all-reduce(f32[64,4,1024]{2,0,1:T(8,128)} %pad_maximum_fusion), channel_id=1, replica_groups=mesh['seq'=4,'exp'=8] {'seq','exp'}, use_global_device_ids=true, to_apply=%region_6.0 | all-reduce | flops 262144 | bytes 1572864 | tf_op jit(solution)/shard_map/psum | solution.py:25
  158.4 3.5 fusion.38
  162.0 3.5 fusion.28
  170.1 4.0 convolution_convert_fusion.3
  177.0 4.2 convolution_convert_fusion
  181.2 3.3 convolution_convert_fusion.1
  184.5 33.1 %all-reduce.4.cloned.1.call-done = (bf16[8,2,1024]{2,0,1:T(8,128)(2,1)}, bf16[8,2,1024]{2,0,1:T(8,128)(2,1)}) async-done(((bf16[8,2,1024]{2,0,1:T(8,128)(2,1)}, bf16[8,2,1024]{2,0,1:T(8,128)(2,1)}), (bf16[8,2,1024]{2,0,1:T(8,128)(2,1)}, bf16[8,2,1024]{2,0,1:T(8,128)(2,1)})) %all-reduce.4.cloned.1.call-update) | async-done | bytes 65552 | tf_op jit(solution)/shard_map/psum | solution.py:46
  217.6 14.6 %all_gather.13 = bf16[64,2,1024]{2,0,1:T(8,128)(2,1)S(1)} all-gather(bf16[8,2,1024]{2,0,1:T(8,128)(2,1)} %get-tuple-element.21), channel_id=1, replica_groups=mesh['seq'=4,'exp'=8] {'exp'}, dimensions={0}, use_global_device_ids=true | all-gather | bytes 294912 | tf_op jit(solution)/shard_map/all_gather | solution.py:57
  232.2 3.8 fusion.17
  236.0 1.8 multiply_reduce_fusion.1
  237.8 14.2 %all_gather.12 = bf16[64,2,1024]{2,0,1:T(8,128)(2,1)S(1)} all-gather(bf16[8,2,1024]{2,0,1:T(8,128)(2,1)S(1)} %copy-done.8), channel_id=1, replica_groups=mesh['seq'=4,'exp'=8] {'exp'}, dimensions={0}, use_global_device_ids=true | all-gather | bytes 294912 | tf_op jit(solution)/shard_map/all_gather | solution.py:51
  252.1 1.8 convolution_bitcast_fusion.2
  253.9 43.1 %all-gather.1 = f32[32,2,64]{2,1,0:T(2,128)} all-gather(f32[1,2,64]{2,1,0:T(2,128)S(1)} %bitcast.44), channel_id=2, replica_groups=mesh['seq'=4,'exp'=8] {'seq','exp'}, dimensions={0}, use_global_device_ids=true | all-gather | bytes 16896 | tf_op jit(solution)/shard_map/all_gather | solution.py:61
  298.4 3.0 convolution_bitcast_fusion.4
  301.4 2.0 copy.23
  303.4 3.7 convolution_convert_fusion.2
  307.0 6.2 %add_convert_fusion = bf16[2,768,1024]{2,1,0:T(8,128)(2,1)} fusion(f32[2,768,1024]{2,1,0:T(8,128)} %fusion.17, f32[2,768,64]{1,2,0:T(8,128)} %convolution_bitcast_fusion.2, f32[2,768,64]{1,2,0:T(8,128)} %get-tuple-element.31, f32[2,64]{1,0:T(2,128)} %reduce_sum.48, bf16[1024,64]{0,1:T(8,128)(2,1)} %param.6, f32[2,768,64]{1,2,0:T(8,128)} %get-tuple-element.25, ...), kind=kOutput, calls=%fused_computation.2 | convolution fusion | flops 205555264 | bytes 11148800 | tf_op jit(solution)/shard_map/dot_general | solution.py:66
  313.3 123.1 %reduce-scatter.4.cloned.1.call-done = f32[32,64]{1,0:T(8,128)} async-done(((f32[1024,64]{1,0:T(8,128)}), f32[32,64]{1,0:T(8,128)}) %reduce-scatter.4.cloned.1.call-update) | async-done | bytes 8208
  (36 shorter events, 18.3 us)
Async XLA Ops:
  7.2 1.9 copy-start
  7.2 210.4 %all-reduce.4.cloned.1.call-start = ((), (), s32[]{:S(2)}) async-start(), calls=%async_computation.2 | async-start | bytes 131072 | tf_op jit(solution)/shard_map/psum | solution.py:46
  158.4 3.5 copy-start.6
  158.4 7.7 %copy-start.1 = (bf16[2,1024,1024]{2,1,0:T(8,128)(2,1)S(1)}, bf16[2,1024,1024]{2,1,0:T(8,128)(2,1)}, u32[]{:S(2)}) copy-start(bf16[2,1024,1024]{2,1,0:T(8,128)(2,1)} %param.8) | copy-start | bytes 12582916
  165.5 0.6 copy-start.4
  176.9 259.4 %reduce-scatter.4.cloned.1.call-start = ((), (), s32[]{:S(2)}) async-start(), calls=%async_computation.1 | async-start | bytes 540672
  177.0 4.2 copy-start.5
  177.0 4.2 copy-start.7
  232.2 5.6 %copy-start.8 = (bf16[8,2,1024]{2,0,1:T(8,128)(2,1)S(1)}, bf16[8,2,1024]{2,0,1:T(8,128)(2,1)}, u32[]{:S(2)}) copy-start(bf16[8,2,1024]{2,0,1:T(8,128)(2,1)} %get-tuple-element.20) | copy-start | bytes 98308
  232.2 19.8 %copy-start.2 = (bf16[2,768,1024]{2,1,0:T(8,128)(2,1)S(1)}, bf16[2,768,1024]{2,1,0:T(8,128)(2,1)}, u32[]{:S(2)}) copy-start(bf16[2,768,1024]{2,1,0:T(8,128)(2,1)} %param.9) | copy-start | bytes 9437188
  252.1 1.8 copy-start.3
Sparse Core Ops, SparseCore 0:
  177.0 40.5 all-reduce.3
  303.5 132.8 reduce-scatter.3
